TPU v7x, 32 devices: a whole 2x2x4 slice. The times are simulated.
32 devices in a mesh: cond: 2 (over core), kern: 2 (over y), tile: 8 (over z, x).
Axes of the slice: x: 2, y: 2, z: 4, core: 2. Of those that a mesh axis runs over, the one named last changes fastest.
Arguments:
- mask: bfloat16 [1, 1024, 1024], P(None, 'tile'), may hold values from -6 to 6
- kernels: bfloat16 [2, 4, 24, 512, 512], P(None, 'cond', 'kern', 'tile'), may hold values from -6 to 6
- kernel_weights: float32 [4, 24], P('cond', 'kern'), may hold values from 0.02 to 0.2
Outputs:
- low: float32 [1, 1024, 1024], P(None, 'tile', 'kern')
- high: float32 [1, 1024, 1024], P(None, 'tile', 'kern')
All inputs are finite; a program needn't handle non-finite values.
Results may differ from a plain program's by a relative error of at most 0.0032.
Values may be sent and summed in bfloat16 or wider, within the bound.
A program may use at most 128 MiB of HBM per device.

v0:
```python
import math

import jax
import jax.numpy as jnp
from jax import lax
from jax.sharding import PartitionSpec as P


def tables(length, count):
    pixel = jnp.arange(length, dtype=jnp.int32)[:, None]
    freq = jnp.arange(count, dtype=jnp.int32)[None, :] - count // 2
    phase = jnp.mod(pixel * freq, length).astype(jnp.float32) * (2.0 * math.pi / length)
    factor = 1.0 / math.sqrt(length)
    return (
        (jnp.cos(phase) * factor).astype(jnp.bfloat16),
        (jnp.sin(phase) * factor).astype(jnp.bfloat16),
    )


def field_power(half_re, half_im, cos_table, sin_table):
    field_re = jnp.einsum("tnjr,pj->tnrp", half_re, cos_table, preferred_element_type=jnp.float32)
    field_re = field_re - jnp.einsum(
        "tnjr,pj->tnrp", half_im, sin_table, preferred_element_type=jnp.float32
    )
    field_im = jnp.einsum("tnjr,pj->tnrp", half_re, sin_table, preferred_element_type=jnp.float32)
    field_im = field_im + jnp.einsum(
        "tnjr,pj->tnrp", half_im, cos_table, preferred_element_type=jnp.float32
    )
    return field_re * field_re + field_im * field_im


def filter_spectrum(spec_re, spec_im, kern_re, kern_im):
    kern_re = kern_re.astype(jnp.float32)
    kern_im = kern_im.astype(jnp.float32)
    filt_re = spec_re[:, None] * kern_re[None] - spec_im[:, None] * kern_im[None]
    filt_im = spec_re[:, None] * kern_im[None] + spec_im[:, None] * kern_re[None]
    return (filt_re.astype(jnp.bfloat16), filt_im.astype(jnp.bfloat16))


def half_transform(filt_re, filt_im, cos_part, sin_part):
    half_re = jnp.einsum("tnji,ri->tnjr", filt_re, cos_part, preferred_element_type=jnp.float32)
    half_re = half_re - jnp.einsum(
        "tnji,ri->tnjr", filt_im, sin_part, preferred_element_type=jnp.float32
    )
    half_im = jnp.einsum("tnji,ri->tnjr", filt_re, sin_part, preferred_element_type=jnp.float32)
    half_im = half_im + jnp.einsum(
        "tnji,ri->tnjr", filt_im, cos_part, preferred_element_type=jnp.float32
    )
    return (half_re.astype(jnp.bfloat16), half_im.astype(jnp.bfloat16))


def column_spectrum(rows_re, rows_im, cos_part, sin_part):
    spec_re = jnp.einsum("tjr,ri->tji", rows_re, cos_part, preferred_element_type=jnp.float32)
    spec_re = spec_re + jnp.einsum(
        "tjr,ri->tji", rows_im, sin_part, preferred_element_type=jnp.float32
    )
    spec_im = jnp.einsum("tjr,ri->tji", rows_im, cos_part, preferred_element_type=jnp.float32)
    spec_im = spec_im - jnp.einsum(
        "tjr,ri->tji", rows_re, sin_part, preferred_element_type=jnp.float32
    )
    return (spec_re, spec_im)


def local(mask, kernels, kernel_weights):
    tiles_here, rows, pixels = mask.shape
    count = kernels.shape[4]
    conds, kerns = kernel_weights.shape
    items = conds * kerns
    cos_table, sin_table = tables(pixels, count)
    row_re = jnp.einsum("trc,cj->tjr", mask, cos_table, preferred_element_type=jnp.float32).astype(
        jnp.bfloat16
    )
    row_im = (
        -jnp.einsum("trc,cj->tjr", mask, sin_table, preferred_element_type=jnp.float32)
    ).astype(jnp.bfloat16)
    cols_re, cols_im = (
        lax.all_to_all(row_re, "tile", split_axis=1, concat_axis=2, tiled=True),
        lax.all_to_all(row_im, "tile", split_axis=1, concat_axis=2, tiled=True),
    )
    spec_re, spec_im = column_spectrum(cols_re, cols_im, cos_table, sin_table)
    freq_here = kernels.shape[3]
    kern_re = kernels[0].reshape(items, freq_here, count)
    kern_im = kernels[1].reshape(items, freq_here, count)
    filt_re, filt_im = filter_spectrum(spec_re, spec_im, kern_re, kern_im)
    half_re, half_im = half_transform(filt_re, filt_im, cos_table, sin_table)
    power = field_power(
        lax.all_to_all(half_re, "tile", split_axis=3, concat_axis=2, tiled=True),
        lax.all_to_all(half_im, "tile", split_axis=3, concat_axis=2, tiled=True),
        cos_table,
        sin_table,
    )
    power = power.reshape(tiles_here, conds, kerns, rows, pixels)
    weighted = jnp.einsum("tckrp,ck->tcrp", power, kernel_weights, precision=lax.Precision.HIGHEST)
    intensity = lax.psum_scatter(weighted, "kern", scatter_dimension=3, tiled=True)
    local_low = jnp.min(intensity, axis=1)
    local_high = jnp.max(intensity, axis=1)
    low = lax.pmin(local_low, "cond")
    high = lax.pmax(local_high, "cond")
    return (low, high)


def solution(mesh):
    placed = (P(None, "tile", None), P(None, "cond", "kern", "tile", None), P("cond", "kern"))
    return jax.shard_map(
        local,
        mesh=mesh,
        in_specs=placed,
        out_specs=(P(None, "tile", "kern"), P(None, "tile", "kern")),
        check_vma=False,
    )
```

profile of v0, /device:TPU:0, one launch (start us, length us, event | category | flops | bytes accessed | tf_op | source)
XLA Modules:
  0.0 441.4 jit_solution(14365424099904626145)
XLA Ops:
  8.1 8.2 %fusion.16 = bf16[1,512,128]{2,1,0:T(8,128)(2,1)S(1)} fusion(s32[512]{0:T(512)S(1)} %iota_add_fusion, bf16[1,128,1024]{2,1,0:T(8,128)(2,1)S(1)} %copy-done), kind=kOutput, calls=%fused_computation.30 | convolution fusion | flops 142737408 | bytes 395264 | tf_op jit(solution)/shard_map/trc,cj->tjr/dot_general | solution.py:74
  26.4 8.1 %fusion.15 = bf16[1,512,128]{2,1,0:T(8,128)(2,1)S(1)} fusion(s32[512]{0:T(512)S(1)} %iota_add_fusion, bf16[1,128,1024]{2,1,0:T(8,128)(2,1)S(1)} %copy-done), kind=kOutput, calls=%fused_computation.29 | convolution fusion | flops 142671872 | bytes 395264 | tf_op jit(solution)/shard_map/trc,cj->tjr/dot_general | solution.py:70
  39.0 17.6 %all-to-all-start = ((bf16[8,2,4096]{2,1,0:T(2,128)(2,1)}), bf16[8,2,4096]{2,1,0:T(2,128)(2,1)}, u32[]{:S(2)}, u32[]{:S(2)}) async-start(bf16[8,2,4096]{2,1,0:T(2,128)(2,1)} %reshape.127), calls=%async_computation | async-start | bytes 262144 | tf_op jit(solution)/shard_map/all_to_all | solution.py:77
  56.9 8.6 %fusion.30 = f32[64,512]{1,0:T(8,128)} fusion(s32[512]{0:T(512)S(1)} %iota_add_fusion, bf16[8,8,8,128]{3,2,1,0:T(8,128)(2,1)S(1)} %bitcast.118), kind=kOutput, calls=%fused_computation.47 | convolution fusion | flops 75497472 | bytes 264192 | tf_op jit(solution)/shard_map/tjr,ri->tji/dot_general | solution.py:57
  74.9 8.3 %convolution_subtract_fusion = f32[64,512]{1,0:T(8,128)S(1)} fusion(f32[64,512]{1,0:T(8,128)S(1)} %copy-done.7, s32[512]{0:T(512)S(1)} %iota_add_fusion, bf16[8,8,8,128]{3,2,1,0:T(8,128)(2,1)S(1)} %bitcast.121), kind=kOutput, calls=%fused_computation.31 | convolution fusion | flops 75530240 | bytes 395264 | tf_op jit(solution)/shard_map/tjr,ri->tji/dot_general | solution.py:58
  83.1 8.0 %convolution_add_fusion = f32[64,512]{1,0:T(8,128)S(1)} fusion(f32[64,512]{1,0:T(8,128)S(1)} %fusion.31, s32[512]{0:T(512)S(1)} %iota_add_fusion, bf16[8,8,8,128]{3,2,1,0:T(8,128)(2,1)S(1)} %bitcast.119), kind=kOutput, calls=%fused_computation.32 | convolution fusion | flops 75530240 | bytes 395264 | tf_op jit(solution)/shard_map/tjr,ri->tji/dot_general | solution.py:54
  92.4 8.7 %fusion.28 = f32[24,64,1024]{2,1,0:T(8,128)S(1)} fusion(bf16[24,64,512]{2,1,0:T(8,128)(2,1)S(1)} %get-tuple-element.5, s32[512]{0:T(512)S(1)} %iota_add_fusion), kind=kOutput, calls=%fused_computation.44 | convolution fusion | flops 1619001344 | bytes 7866368 | tf_op jit(solution)/shard_map/tnji,ri->tnjr/dot_general | solution.py:41
  101.1 12.2 %fusion.6 = bf16[1,24,64,1024]{3,2,1,0:T(8,128)(2,1)S(1)} fusion(f32[24,64,1024]{2,1,0:T(8,128)S(1)} %fusion.28, bf16[24,64,512]{2,1,0:T(8,128)(2,1)S(1)} %get-tuple-element.4, s32[512]{0:T(512)S(1)} %iota_add_fusion), kind=kOutput, calls=%fused_computation.13 | convolution fusion | flops 1622147072 | bytes 11012096 | tf_op jit(solution)/shard_map/tnji,ri->tnjr/dot_general | solution.py:42
  120.0 8.9 %reshape.129 = bf16[8,2,98304]{2,1,0:T(2,128)(2,1)} reshape(bf16[1024,1,24,64]{3,2,1,0:T(8,128)(2,1)} %bitcast.97) | data formatting | bytes 6291456
  134.9 10.3 %fusion.21 = f32[24,64,1024]{2,1,0:T(8,128)S(1)} fusion(bf16[24,64,512]{2,1,0:T(8,128)(2,1)} %copy-done.5, s32[512]{0:T(512)S(1)} %iota_add_fusion), kind=kOutput, calls=%fused_computation.37 | convolution fusion | flops 1619001344 | bytes 7866368 | tf_op jit(solution)/shard_map/tnji,ri->tnjr/dot_general | solution.py:45
  145.3 10.8 %fusion.7 = bf16[1,24,64,1024]{3,2,1,0:T(8,128)(2,1)} fusion(f32[24,64,1024]{2,1,0:T(8,128)S(1)} %fusion.21, bf16[24,64,512]{2,1,0:T(8,128)(2,1)S(1)} %copy-done.4, s32[512]{0:T(512)S(1)} %iota_add_fusion), kind=kOutput, calls=%fused_computation.14 | convolution fusion | flops 1622147072 | bytes 11012096 | tf_op jit(solution)/shard_map/tnji,ri->tnjr/dot_general | solution.py:46
  156.1 7.9 %copy.47 = bf16[1,24,64,1024]{2,1,0,3:T(8,128)(2,1)} copy(bf16[1,24,64,1024]{3,2,1,0:T(8,128)(2,1)} %fusion.7) | data formatting | bytes 6291456 | tf_op jit(solution)/shard_map/convert_element_type | solution.py:49
  164.0 9.1 %reshape.131 = bf16[8,2,98304]{2,1,0:T(2,128)(2,1)} reshape(bf16[1024,1,24,64]{3,2,1,0:T(8,128)(2,1)} %bitcast.98) | data formatting | bytes 6291456
  173.1 31.4 %all-to-all-done.2 = bf16[8,2,98304]{2,1,0:T(2,128)(2,1)S(1)} async-done(((bf16[8,2,98304]{2,1,0:T(2,128)(2,1)}), bf16[8,2,98304]{2,1,0:T(2,128)(2,1)S(1)}, u32[]{:S(2)}, u32[]{:S(2)}) %all-to-all-start.2) | async-done | bytes 3145760 | tf_op jit(solution)/shard_map/all_to_all | solution.py:87
  222.5 13.3 %fusion.17 = f32[24,128,1024]{2,1,0:T(8,128)} fusion(bf16[24,512,128]{2,1,0:T(8,128)(2,1)S(1)} %bitcast.108, s32[512]{0:T(512)S(1)} %iota_add_fusion), kind=kOutput, calls=%fused_computation.33 | convolution fusion | flops 3229614080 | bytes 15730688 | tf_op jit(solution)/shard_map/tnjr,pj->tnrp/dot_general | solution.py:25
  235.8 13.3 %fusion.26 = f32[24,128,1024]{2,1,0:T(8,128)} fusion(bf16[24,512,128]{2,1,0:T(8,128)(2,1)S(1)} %bitcast.109, s32[512]{0:T(512)S(1)} %iota_add_fusion), kind=kOutput, calls=%fused_computation.42 | convolution fusion | flops 3229614080 | bytes 15730688 | tf_op jit(solution)/shard_map/tnjr,pj->tnrp/dot_general | solution.py:21
  249.1 30.1 %all-to-all-done.3 = bf16[8,2,98304]{2,1,0:T(2,128)(2,1)} async-done(((bf16[8,2,98304]{2,1,0:T(2,128)(2,1)}), bf16[8,2,98304]{2,1,0:T(2,128)(2,1)}, u32[]{:S(2)}, u32[]{:S(2)}) %all-to-all-start.3) | async-done | bytes 3145760 | tf_op jit(solution)/shard_map/all_to_all | solution.py:88
  279.2 8.8 %reshape.132 = bf16[1024,1,24,64]{3,2,1,0:T(8,128)(2,1)} reshape(bf16[8,2,98304]{2,1,0:T(2,128)(2,1)} %all-to-all-done.3) | data formatting | bytes 6291456
  296.9 13.6 %fusion.19 = f32[24,128,1024]{2,1,0:T(8,128)} fusion(bf16[24,512,128]{2,1,0:T(8,128)(2,1)S(1)} %bitcast.105, s32[512]{0:T(512)S(1)} %iota_add_fusion), kind=kOutput, calls=%fused_computation.35 | convolution fusion | flops 3229614080 | bytes 15730688 | tf_op jit(solution)/shard_map/tnjr,pj->tnrp/dot_general | solution.py:22
  310.5 31.1 %multiply_add_fusion = f32[24,128,1024]{2,1,0:T(8,128)S(1)} fusion(f32[24,128,1024]{2,1,0:T(8,128)S(1)} %bitcast.104, f32[24,128,1024]{2,1,0:T(8,128)} %fusion.26, f32[24,128,1024]{2,1,0:T(8,128)} %fusion.19, bf16[24,512,128]{2,1,0:T(8,128)(2,1)} %bitcast.106, s32[512]{0:T(512)S(1)} %iota_add_fusion), kind=kOutput, calls=%fused_computation.2 | convolution fusion | flops 3245342720 | bytes 53479424 | tf_op jit(solution)/shard_map/tnjr,pj->tnrp/dot_general | solution.py:26
  341.7 25.2 %fusion = f32[2,1,128,1024]{3,1,2,0:T(1,128)S(1)} fusion(f32[2,12,1,1]{1,2,3,0:T(1,128)S(1)} %bitcast.122, f32[2,12,128,1024]{3,2,1,0:T(8,128)S(1)} %bitcast.96), kind=kOutput, calls=%fused_computation | convolution fusion | flops 37748736 | bytes 13631584 | tf_op jit(solution)/shard_map/tckrp,ck->tcrp/dot_general | solution.py:93
  368.1 19.6 %reduce-scatter.2.cloned.1.call-done = f32[1,2,128,512]{3,2,1,0:T(8,128)} async-done(((f32[1,2,128,1024]{3,2,1,0:T(8,128)}), f32[1,2,128,512]{3,2,1,0:T(8,128)}) %reduce-scatter.2.cloned.1.call-update) | async-done | bytes 524304 | tf_op jit(solution)/shard_map/reduce_scatter | solution.py:94
  390.4 18.4 %all-reduce.3.cloned.1.call-done = f32[1,128,512]{2,1,0:T(8,128)} async-done(((f32[1,128,512]{2,1,0:T(8,128)}), f32[1,128,512]{2,1,0:T(8,128)}) %all-reduce.3.cloned.1.call-update) | async-done | bytes 262160 | tf_op jit(solution)/shard_map/pmin | solution.py:97
  408.7 22.3 %all-reduce.5.cloned.1.call-done = f32[1,128,512]{2,1,0:T(8,128)} async-done(((f32[1,128,512]{2,1,0:T(8,128)}), f32[1,128,512]{2,1,0:T(8,128)}) %all-reduce.5.cloned.1.call-update) | async-done | bytes 262160 | tf_op jit(solution)/shard_map/pmax | solution.py:98
  (61 shorter events, 73.0 us)
Async XLA Ops:
  7.2 1.0 copy-start
  19.2 19.9 %all-to-all-start.1 = ((bf16[8,2,4096]{2,1,0:T(2,128)(2,1)}), bf16[8,2,4096]{2,1,0:T(2,128)(2,1)S(1)}, u32[]{:S(2)}, u32[]{:S(2)}) async-start(bf16[8,2,4096]{2,1,0:T(2,128)(2,1)} %reshape.125), calls=%async_computation.1 | async-start | bytes 262144 | tf_op jit(solution)/shard_map/all_to_all | solution.py:78
  39.0 26.5 %all-to-all-start = ((bf16[8,2,4096]{2,1,0:T(2,128)(2,1)}), bf16[8,2,4096]{2,1,0:T(2,128)(2,1)}, u32[]{:S(2)}, u32[]{:S(2)}) async-start(bf16[8,2,4096]{2,1,0:T(2,128)(2,1)} %reshape.127), calls=%async_computation | async-start | bytes 262144 | tf_op jit(solution)/shard_map/all_to_all | solution.py:77
  67.1 7.8 %copy-start.7 = (f32[64,512]{1,0:T(8,128)S(1)}, f32[64,512]{1,0:T(8,128)}, u32[]{:S(2)}) copy-start(f32[64,512]{1,0:T(8,128)} %fusion.30) | copy-start | bytes 393220
  92.4 8.8 %copy-start.5 = (bf16[24,64,512]{2,1,0:T(8,128)(2,1)}, bf16[24,64,512]{2,1,0:T(8,128)(2,1)S(1)}, u32[]{:S(2)}) copy-start(bf16[24,64,512]{2,1,0:T(8,128)(2,1)S(1)} %get-tuple-element.5) | copy-start | bytes 4718596
  92.4 8.8 %copy-start.3 = (bf16[24,64,512]{2,1,0:T(8,128)(2,1)}, bf16[24,64,512]{2,1,0:T(8,128)(2,1)S(1)}, u32[]{:S(2)}) copy-start(bf16[24,64,512]{2,1,0:T(8,128)(2,1)S(1)} %get-tuple-element.4) | copy-start | bytes 4718596
  128.9 75.6 %all-to-all-start.2 = ((bf16[8,2,98304]{2,1,0:T(2,128)(2,1)}), bf16[8,2,98304]{2,1,0:T(2,128)(2,1)S(1)}, u32[]{:S(2)}, u32[]{:S(2)}) async-start(bf16[8,2,98304]{2,1,0:T(2,128)(2,1)} %reshape.129), calls=%async_computation.2 | async-start | bytes 6291456 | tf_op jit(solution)/shard_map/all_to_all | solution.py:87
  134.9 10.4 %copy-start.4 = (bf16[24,64,512]{2,1,0:T(8,128)(2,1)S(1)}, bf16[24,64,512]{2,1,0:T(8,128)(2,1)}, u32[]{:S(2)}) copy-start(bf16[24,64,512]{2,1,0:T(8,128)(2,1)} %copy-done.3) | copy-start | bytes 4718596
  204.5 74.6 %all-to-all-start.3 = ((bf16[8,2,98304]{2,1,0:T(2,128)(2,1)}), bf16[8,2,98304]{2,1,0:T(2,128)(2,1)}, u32[]{:S(2)}, u32[]{:S(2)}) async-start(bf16[8,2,98304]{2,1,0:T(2,128)(2,1)} %reshape.131), calls=%async_computation.3 | async-start | bytes 6291456 | tf_op jit(solution)/shard_map/all_to_all | solution.py:88
  209.0 178.7 %reduce-scatter.2.cloned.1.call-start = ((), (), s32[]{:S(2)}) async-start(), calls=%async_computation.5 | async-start | bytes 1572864 | tf_op jit(solution)/shard_map/reduce_scatter | solution.py:94
  294.4 16.1 %slice-start = ((s8[12582912]{0:T(1024)(128)(4,1)}), s8[4194304]{0:T(1024)(128)(4,1)S(1)}, s32[]{:S(2)}) async-start(s8[12582912]{0:T(1024)(128)(4,1)} %bitcast.103), calls=%async_computation.8 | async-start | bytes 8388608
  295.3 1.6 copy-start.2
  296.9 13.6 %slice-start.1 = ((s8[12582912]{0:T(1024)(128)(4,1)}), s8[4194304]{0:T(1024)(128)(4,1)S(1)}, s32[]{:S(2)}) async-start(s8[12582912]{0:T(1024)(128)(4,1)} %bitcast.103), calls=%async_computation.9 | async-start | bytes 8388608
  296.9 13.6 %slice-start.2 = ((s8[12582912]{0:T(1024)(128)(4,1)}), s8[4194304]{0:T(1024)(128)(4,1)S(1)}, s32[]{:S(2)}) async-start(s8[12582912]{0:T(1024)(128)(4,1)} %bitcast.103), calls=%async_computation.10 | async-start | bytes 8388608
  310.5 31.1 %copy-start.6 = (f32[2,12]{1,0:T(2,128)S(1)}, f32[2,12]{1,0:T(2,128)}, u32[]{:S(2)}) copy-start(f32[2,12]{1,0:T(2,128)} %param.5) | copy-start | bytes 292
  366.8 67.6 %copy-start.1 = (bf16[1,128,1024]{2,1,0:T(8,128)(2,1)S(1)}, bf16[1,128,1024]{2,1,0:T(8,128)(2,1)}, u32[]{:S(2)}) copy-start(bf16[1,128,1024]{2,1,0:T(8,128)(2,1)} %param.3) | copy-start | bytes 786436
  368.0 40.7 %all-reduce.3.cloned.1.call-start = ((), (), s32[]{:S(2)}) async-start(), calls=%async_computation.6 | async-start | bytes 524288 | tf_op jit(solution)/shard_map/pmin | solution.py:97
  389.6 41.5 %all-reduce.5.cloned.1.call-start = ((), (), s32[]{:S(2)}) async-start(), calls=%async_computation.7 | async-start | bytes 524288 | tf_op jit(solution)/shard_map/pmax | solution.py:98
Sparse Core Ops, SparseCore 0:
  368.2 19.4 reduce-scatter.1
  390.5 18.1 all-reduce.2
  411.6 19.3 all-reduce.4
where the time goes:
time: 449 us; the launch traced here: 441 us
  matrix products  188 us (42%)
  waiting for transfers between devices  122 us (27%)
  local copies, waits for them, and re-layouts  75.3 us (17%)
  starting transfers between devices  35.5 us (8%)
  between operations  14.5 us (3%)
  other arithmetic  5.97 us (1%)
    unnamed x35, local copies, waits for them, and re-layouts  42.3 us
    all_to_all x1, waiting for transfers between devices, local(): lax.all_to_all(half_re, 'tile', split_axis=3, concat_axis=2, tiled=True)  31.4 us
    dot_general x1, matrix products, field_power(): jnp.einsum('tnjr,pj->tnrp', half_im, cos_table, preferred_element_type=jn...  31.1 us
    all_to_all x1, waiting for transfers between devices, local(): lax.all_to_all(half_im, 'tile', split_axis=3, concat_axis=2, tiled=True)  30.1 us
    dot_general x1, matrix products, local(): jnp.einsum('tckrp,ck->tcrp', power, kernel_weights, precision=lax.Precisi...  25.2 us
    pmax x1, waiting for transfers between devices, local(): high = lax.pmax(local_high, 'cond')  22.3 us
    reduce_scatter x1, waiting for transfers between devices, local(): lax.psum_scatter(weighted, 'kern', scatter_dimension=3, tiled=True)  19.6 us
    pmin x1, waiting for transfers between devices, local(): low = lax.pmin(local_low, 'cond')  18.4 us
  transfers between devices with their start and end apart: 7, of which 5 were waited for; matrix products, arithmetic and copies ran while one was open for 23% of the time, Pallas kernels for 0%

commit v1 on v0

--- a/solution.py
+++ b/solution.py
@@ -1,8 +1,12 @@
+import functools
 import math
 
 import jax
 import jax.numpy as jnp
+import numpy as np
 from jax import lax
+from jax.experimental import pallas as pl
+from jax.experimental.pallas import tpu as pltpu
 from jax.sharding import PartitionSpec as P
 
 
@@ -99,10 +103,279 @@
     return (low, high)
 
 
+def host_tables(length, count):
+    pixel = np.arange(length, dtype=np.int64)[:, None]
+    freq = np.arange(count, dtype=np.int64)[None, :] - count // 2
+    phase = np.mod(pixel * freq, length).astype(np.float64) * (2.0 * math.pi / length)
+    factor = 1.0 / math.sqrt(length)
+    return np.cos(phase) * factor, np.sin(phase) * factor
+
+
+def filter_kernel(core_ref, spec_ref, kept_ref, came_ref, out_ref):
+    freqs, count = spec_ref.shape[1:]
+    half = freqs // 2
+    row = lax.broadcasted_iota(jnp.int32, (freqs, freqs), 0)
+    col = lax.broadcasted_iota(jnp.int32, (freqs, freqs), 1)
+    source = jnp.where(row < half, 2 * row, 2 * (row - half) + 1)
+    order = (col == source).astype(jnp.bfloat16)
+    spec_re = spec_ref[0]
+    spec_im = spec_ref[1]
+
+    def apply(kern_ref):
+        chunks = kern_ref.shape[2]
+        for part in range(kern_ref.shape[1] * chunks):
+            kern_re = kern_ref[0, part // chunks, part % chunks].astype(jnp.float32)
+            kern_im = kern_ref[1, part // chunks, part % chunks].astype(jnp.float32)
+            filt_re = (spec_re * kern_re - spec_im * kern_im).astype(jnp.bfloat16)
+            filt_im = (spec_re * kern_im + spec_im * kern_re).astype(jnp.bfloat16)
+            out_ref[part, 0] = jnp.dot(order, filt_re, preferred_element_type=jnp.float32).astype(
+                jnp.bfloat16
+            )
+            out_ref[part, 1] = jnp.dot(order, filt_im, preferred_element_type=jnp.float32).astype(
+                jnp.bfloat16
+            )
+
+    mine = pl.program_id(0) == core_ref[0]
+
+    @pl.when(mine)
+    def _():
+        apply(kept_ref)
+
+    @pl.when(jnp.logical_not(mine))
+    def _():
+        apply(came_ref)
+
+
+def filter_round(core, spec, kernels, came, which):
+    _, conds, _, chunks, _, freqs, count = kernels.shape
+    owners = conds * chunks
+    mine = pl.BlockSpec(
+        (2, conds, None, chunks, None, freqs, count),
+        lambda b, own: (0, 0, own[0], 0, which, 0, 0),
+    )
+    theirs = pl.BlockSpec(
+        (2, conds, chunks, None, freqs, count), lambda b, own: (0, 0, 0, which, 0, 0)
+    )
+    return pl.pallas_call(
+        filter_kernel,
+        grid_spec=pltpu.PrefetchScalarGridSpec(
+            num_scalar_prefetch=1,
+            grid=(2,),
+            in_specs=[pl.BlockSpec((2, freqs, count), lambda b, own: (0, 0, 0)), mine, theirs],
+            out_specs=pl.BlockSpec((owners, 2, freqs, count), lambda b, own: (b, 0, 0, 0)),
+        ),
+        out_shape=jax.ShapeDtypeStruct((2 * owners, 2, freqs, count), jnp.bfloat16),
+        cost_estimate=pl.CostEstimate(
+            flops=32 * owners * freqs * freqs * count,
+            bytes_accessed=16 * owners * freqs * count,
+            transcendentals=0,
+        ),
+    )(core, spec, kernels, came)
+
+
+def item_kernel(first, last, weight_ref, parts_ref, wave_ref, back_ref, *rest):
+    if first:
+        out_ref, mixed, turn = rest
+        sum_ref = None
+    else:
+        sum_ref, out_ref, mixed, turn = rest
+    owners, _, freqs, count = parts_ref.shape
+    half = freqs // 2
+    quarter = count // 2
+    width = back_ref.shape[2]
+
+    @pl.when(pl.program_id(0) == 0)
+    def _():
+        for parity in range(2):
+            base = parity * count
+            for owner in range(owners):
+                at = base + owner * half
+                re = parts_ref[owner, 0, parity * half : (parity + 1) * half, :]
+                im = parts_ref[owner, 1, parity * half : (parity + 1) * half, :]
+                mixed[at : at + half, :count] = re
+                mixed[at : at + half, count:] = -im
+                mixed[at + quarter : at + quarter + half, :count] = im
+                mixed[at + quarter : at + quarter + half, count:] = re
+            cos_part = back_ref[2 * parity]
+            sin_part = back_ref[2 * parity + 1]
+            turn[parity, :quarter, :width] = cos_part
+            turn[parity, :quarter, width:] = sin_part
+            turn[parity, quarter:, :width] = -sin_part
+            turn[parity, quarter:, width:] = cos_part
+
+    halves = lax.dot_general(
+        wave_ref[...], mixed[...], (((1,), (1,)), ((), ())), preferred_element_type=jnp.float32
+    ).astype(jnp.bfloat16)
+    even = jnp.dot(halves[:, :count], turn[0], preferred_element_type=jnp.float32)
+    odd = jnp.dot(halves[:, count:], turn[1], preferred_element_type=jnp.float32)
+    near = even + odd
+    far = even - odd
+    weight = weight_ref[0]
+    powers = []
+    for index, field in enumerate((near, far)):
+        re = field[:, :width]
+        im = field[:, width:]
+        power = weight * (re * re + im * im)
+        if not first:
+            power = power + sum_ref[:, index * width : (index + 1) * width]
+        powers.append(power)
+    if not last:
+        for index, power in enumerate(powers):
+            out_ref[:, index * width : (index + 1) * width] = power
+    else:
+        total = jnp.concatenate(powers, axis=1)
+        across, tall, rows, wide = out_ref.shape
+        for k in range(across):
+            for t in range(tall):
+                out_ref[k, t] = total[t * rows : (t + 1) * rows, k * wide : (k + 1) * wide].astype(
+                    out_ref.dtype
+                )
+
+
+def item_round(weight, parts, wave, back, total, last, blocks):
+    pixels = wave.shape[0]
+    owners, _, freqs, count = parts.shape
+    kern, tile = blocks
+    rows = pixels // tile
+    tall = max(1, 256 // rows)
+    step = tall * rows
+    steps = pixels // step
+    first = total is None
+    in_specs = [
+        pl.BlockSpec(memory_space=pltpu.SMEM),
+        pl.BlockSpec(parts.shape, lambda b: (0, 0, 0, 0)),
+        pl.BlockSpec((step, 2 * count), lambda b: (b, 0)),
+        pl.BlockSpec(back.shape, lambda b: (0, 0, 0)),
+    ]
+    args = [weight, parts, wave, back]
+    if not first:
+        in_specs.append(pl.BlockSpec((step, pixels), lambda b: (b, 0)))
+        args.append(total)
+    if last:
+        out_shape = jax.ShapeDtypeStruct((kern, tile, rows, pixels // kern), jnp.bfloat16)
+        out_spec = pl.BlockSpec((kern, tall, rows, pixels // kern), lambda b: (0, b, 0, 0))
+    else:
+        out_shape = jax.ShapeDtypeStruct((pixels, pixels), jnp.float32)
+        out_spec = pl.BlockSpec((step, pixels), lambda b: (b, 0))
+    return pl.pallas_call(
+        functools.partial(item_kernel, first, last),
+        grid=(steps,),
+        out_shape=out_shape,
+        in_specs=in_specs,
+        out_specs=out_spec,
+        scratch_shapes=[
+            pltpu.VMEM((2 * count, 2 * count), jnp.bfloat16),
+            pltpu.VMEM((2, count, pixels), jnp.bfloat16),
+        ],
+        compiler_params=pltpu.CompilerParams(vmem_limit_bytes=48 * 1024 * 1024),
+        cost_estimate=pl.CostEstimate(
+            flops=2 * pixels * 4 * count * count + 4 * pixels * pixels * count,
+            bytes_accessed=4 * pixels * pixels + 4 * owners * freqs * count,
+            transcendentals=0,
+        ),
+    )(*args)
+
+
+def local_items(sizes, mask, kernels, kernel_weights):
+    tile, kern, cond = sizes
+    _, rows, pixels = mask.shape
+    freqs, count = kernels.shape[3:]
+    conds, kerns = kernel_weights.shape
+    items = conds * kerns
+    each = items // tile
+    cos, sin = host_tables(pixels, count)
+    wave = lax.optimization_barrier(
+        jnp.asarray(np.concatenate([cos, sin], axis=1), jnp.bfloat16)
+    )
+    back = jnp.asarray(
+        np.stack([part[: pixels // 2, parity::2].T for parity in range(2) for part in (cos, sin)]),
+        jnp.bfloat16,
+    )
+    me = lax.axis_index("tile")
+    core = lax.axis_index("cond")
+    swap = [(source, 1 - source) for source in range(2)]
+    part = kerns // 2
+    shares = kernels.reshape(2, conds, 2, part // each, each, freqs, count)
+    came = lax.dynamic_index_in_dim(shares, 1 - core, 2, keepdims=False)
+    came = lax.ppermute(came, "cond", swap)
+    other = lax.ppermute(kernel_weights, "cond", swap)
+    weights = jnp.where(
+        core == 0,
+        jnp.concatenate([kernel_weights, other]),
+        jnp.concatenate([other, kernel_weights]),
+    )
+    weights = lax.dynamic_slice(weights, (0, core * part), (2 * conds, part)).reshape(items)
+    weights = lax.dynamic_slice(weights, (me * each,), (each,))
+    row = jnp.dot(mask[0], wave, preferred_element_type=jnp.float32)
+    row = row.reshape(rows, 2, tile, freqs)
+    sign = jnp.asarray([1.0, -1.0], jnp.float32).reshape(1, 2, 1, 1)
+    row = (row * sign).astype(jnp.bfloat16)
+    row = row.transpose(2, 0, 1, 3).reshape(tile, rows, 2 * freqs)
+    cols = lax.all_to_all(row, "tile", split_axis=0, concat_axis=0, tiled=True)
+    cols = cols.reshape(pixels, 2 * freqs)
+    mixed = lax.dot_general(
+        cols, wave, (((0,), (0,)), ((), ())), preferred_element_type=jnp.float32
+    )
+    spec = jnp.stack(
+        [
+            mixed[:freqs, :count] + mixed[freqs:, count:],
+            mixed[freqs:, :count] - mixed[:freqs, count:],
+        ]
+    )
+    arrived = []
+    for index in range(each):
+        sent = filter_round(core.reshape(1), spec, shares, came, index)
+        arrived.append(lax.all_to_all(sent, "tile", split_axis=0, concat_axis=0, tiled=True))
+    total = None
+    for index in range(each):
+        total = item_round(
+            weights[index : index + 1],
+            arrived[index],
+            wave,
+            back,
+            total,
+            index == each - 1,
+            (kern, tile),
+        )
+    wide = pixels // kern
+    total = total.reshape(kern * tile, 2, rows // 2, wide)
+    own = lax.dynamic_index_in_dim(total, core, 1, keepdims=False)
+    sent = lax.dynamic_index_in_dim(total, 1 - core, 1, keepdims=False)
+    got = lax.ppermute(sent, "cond", swap)
+    total = (own.astype(jnp.float32) + got.astype(jnp.float32)).astype(jnp.bfloat16)
+    blocks = lax.all_to_all(total, ("kern", "tile"), split_axis=0, concat_axis=0, tiled=True)
+    blocks = blocks.reshape(kern, 2 * conds, tile // (2 * conds), rows // 2, wide)
+    intensity = jnp.sum(blocks.astype(jnp.float32), axis=(0, 2))
+    both = jnp.stack([jnp.min(intensity, axis=0), jnp.max(intensity, axis=0)])
+    other = lax.ppermute(both, "cond", swap)
+    upper = jnp.where(core == 0, both, other)
+    lower = jnp.where(core == 0, other, both)
+    low = jnp.concatenate([upper[0], lower[0]])
+    high = jnp.concatenate([upper[1], lower[1]])
+    return (low[None], high[None])
+
+
+def plan(mesh):
+    tile, kern, cond = (mesh.shape[name] for name in ("tile", "kern", "cond"))
+
+    def body(mask, kernels, kernel_weights):
+        conds, kerns = kernel_weights.shape
+        freqs = kernels.shape[3]
+        rows, pixels = mask.shape[1:]
+        whole_items = cond == 2 and (conds * kerns) % tile == 0 and tile % (2 * conds) == 0
+        whole_items = whole_items and (kerns // 2) % max(1, conds * kerns // tile) == 0
+        aligned = freqs % 32 == 0 and rows % 32 == 0 and kerns % 2 == 0 and (pixels // kern) % 128 == 0
+        if mask.shape[0] == 1 and whole_items and aligned and kernels.shape[4] * 2 == pixels:
+            return local_items((tile, kern, cond), mask, kernels, kernel_weights)
+        return local(mask, kernels, kernel_weights)
+
+    return body
+
+
 def solution(mesh):
     placed = (P(None, "tile", None), P(None, "cond", "kern", "tile", None), P("cond", "kern"))
     return jax.shard_map(
-        local,
+        plan(mesh),
         mesh=mesh,
         in_specs=placed,
         out_specs=(P(None, "tile", "kern"), P(None, "tile", "kern")),

time: 449 us -> 166 us (0.37); the launches traced: 441 us -> 166 us
  matrix products: 188 us -> 2.77 us
  local copies, waits for them, and re-layouts: 75.3 us -> 7.91 us
  waiting for transfers between devices: 122 us -> 56.2 us
  blocking collectives: 0 us -> 47 us
  Pallas kernels: 0 us -> 34.3 us
  starting transfers between devices: 35.5 us -> 12.8 us
  between operations: 14.5 us -> 0.82 us
    dot_general x15 -> x2, matrix products: 188 us -> 2.77 us  [the longest x1 2.3 us: local_items(): row = jnp.dot(mask[0], wave, preferred_element_type=jnp.float32)]
    all_to_all x0 -> x2, blocking collectives: none -> 47 us  [the longest x1 30.9 us: local_items(): lax.all_to_all(total, ('kern', 'tile'), split_axis=0, concat_axis=0, tile...]
    unnamed x35 -> x12, local copies, waits for them, and re-layouts: 42.3 us -> 1.25 us
    pallas_call x0 -> x6, Pallas kernels: none -> 34.3 us  [the longest x3 25.5 us: item_round(): pl.pallas_call(functools.partial(item_kernel, first, last), grid=(steps,)...]
    all_to_all x4 -> x3, starting transfers between devices: 35.4 us -> 12.1 us  [local_items(): lax.all_to_all(sent, 'tile', split_axis=0, concat_axis=0, tiled=True)]
    pmax x1 -> x0, waiting for transfers between devices: 22.3 us -> none  [local(): high = lax.pmax(local_high, 'cond')]
    reduce_scatter x1 -> x0, waiting for transfers between devices: 19.6 us -> none  [local(): lax.psum_scatter(weighted, 'kern', scatter_dimension=3, tiled=True)]
    pmin x1 -> x0, waiting for transfers between devices: 18.4 us -> none  [local(): low = lax.pmin(local_low, 'cond')]
  transfers between devices with their start and end apart: 7 -> 7, of which waited for: 5 -> 6; matrix products, arithmetic and copies ran while one was open for 23% -> 4% of each run, Pallas kernels for 0% -> 14%
where the time goes in v1:
time: 166 us
  waiting for transfers between devices  56.2 us (34%)
  blocking collectives  47 us (28%)
  Pallas kernels  34.3 us (21%)
  starting transfers between devices  12.8 us (8%)
  local copies, waits for them, and re-layouts  7.91 us (5%)
  other arithmetic  4.02 us (2%)
  matrix products  2.77 us (2%)
    all_to_all x3, waiting for transfers between devices, local_items(): lax.all_to_all(sent, 'tile', split_axis=0, concat_axis=0, tiled=True)  50.8 us
    all_to_all x1, blocking collectives, local_items(): lax.all_to_all(total, ('kern', 'tile'), split_axis=0, concat_axis=0, tile...  30.9 us
    pallas_call x3, Pallas kernels, item_round(): pl.pallas_call(functools.partial(item_kernel, first, last), grid=(steps,)...  25.5 us
    all_to_all x1, blocking collectives, local_items(): cols = lax.all_to_all(row, 'tile', split_axis=0, concat_axis=0, tiled=True)  16.2 us
    all_to_all x3, starting transfers between devices, local_items(): lax.all_to_all(sent, 'tile', split_axis=0, concat_axis=0, tiled=True)  12.1 us
    pallas_call x3, Pallas kernels, filter_round(): pl.pallas_call(filter_kernel, grid_spec=pltpu.PrefetchScalarGridSpec(num_...  8.76 us
  transfers between devices with their start and end apart: 7, of which 6 were waited for; matrix products, arithmetic and copies ran while one was open for 4% of the time, Pallas kernels for 14%

profile of v1, /device:TPU:0, one launch (start us, length us, event | category | flops | bytes accessed | tf_op | source)
XLA Modules:
  0.0 165.8 jit_solution(500392214081863663)
XLA Ops:
  0.7 2.9 %dynamic-slice_bitcast_fusion = bf16[2,2,2,3,64,512]{5,4,3,2,1,0:T(8,128)(2,1)} fusion(bf16[2,2,2,2,3,64,512]{6,5,4,3,2,1,0:T(8,128)(2,1)} %bitcast.49, s32[]{:T(128)S(6)} %select_n.40), kind=kLoop, calls=%fused_computation.3 | loop fusion | bytes 3145732 | tf_op jit(solution)/shard_map/jit(dynamic_index_in_dim)/squeeze | solution.py:299
  4.0 2.6 %copy.14 = bf16[1024,1024]{1,0:T(8,128)(2,1)} copy(bf16[1024,1024]{0,1:T(8,128)(2,1)S(1)} %bitcast.46) | data formatting | bytes 4194304 | tf_op jit(solution)/shard_map/dot_general | solution.py:309
  6.6 2.3 %fusion.2 = bf16[8,128,2,64]{1,3,0,2:T(8,128)(2,1)S(1)} fusion(bf16[2,8,64,1024]{3,2,1,0:T(8,128)(2,1)} %bitcast.54, bf16[1,128,1024]{2,1,0:T(8,128)(2,1)S(1)} %copy-done, f32[2]{0:T(128)S(1)} %copy-done.5), kind=kOutput, calls=%fused_computation.6 | convolution fusion | flops 268697600 | bytes 2621448 | tf_op jit(solution)/shard_map/dot_general | solution.py:309
  8.9 16.2 %all_to_all.25 = bf16[8,128,128]{1,2,0:T(8,128)(2,1)S(1)} all-to-all(bf16[8,128,128]{1,2,0:T(8,128)(2,1)S(1)} %bitcast.59), channel_id=1, replica_groups=mesh['cond'=2,'kern'=2,'tile'=8] {'tile'}, dimensions={0} | all-to-all | bytes 524288 | tf_op jit(solution)/shard_map/all_to_all | solution.py:314
  25.8 0.7 pad_maximum_fusion.spec_ref
  26.5 2.9 %shard_map.79 = bf16[8,2,64,512]{3,2,1,0:T(8,128)(2,1)} custom-call(s32[1]{0:T(128)} %bitcast.core_ref, f32[2,64,512]{2,1,0:T(8,128)} %pad_maximum_fusion.spec_ref, bf16[2,2,2,2,3,64,512]{6,5,4,3,2,1,0:T(8,128)(2,1)} %bitcast.50, bf16[2,2,2,3,64,512]{5,4,3,2,1,0:T(8,128)(2,1)} %collective-permute-done.1.came_ref), custom_call_target="tpu_custom_call" | custom-call | flops 268435456 | bytes 2097152 | tf_op jit(solution)/shard_map/pallas_call | solution.py:159
  29.4 3.6 %all-to-all-start.3 = ((bf16[8,2,64,512]{3,2,1,0:T(8,128)(2,1)}), bf16[8,2,64,512]{3,2,1,0:T(8,128)(2,1)S(1)}, u32[]{:S(2)}, u32[]{:S(2)}) async-start(bf16[8,2,64,512]{3,2,1,0:T(8,128)(2,1)} %shard_map.79), calls=%async_computation.3 | async-start | bytes 2097152 | tf_op jit(solution)/shard_map/all_to_all | solution.py:328
  33.0 2.9 %shard_map.78 = bf16[8,2,64,512]{3,2,1,0:T(8,128)(2,1)} custom-call(s32[1]{0:T(128)} %bitcast.core_ref, f32[2,64,512]{2,1,0:T(8,128)} %pad_maximum_fusion.spec_ref, bf16[2,2,2,2,3,64,512]{6,5,4,3,2,1,0:T(8,128)(2,1)} %bitcast.51, bf16[2,2,2,3,64,512]{5,4,3,2,1,0:T(8,128)(2,1)} %collective-permute-done.1.came_ref), custom_call_target="tpu_custom_call" | custom-call | flops 268435456 | bytes 2097152 | tf_op jit(solution)/shard_map/pallas_call | solution.py:159
  35.9 23.1 %all-to-all-done.3.parts_ref = bf16[8,2,64,512]{3,2,1,0:T(8,128)(2,1)S(1)} async-done(((bf16[8,2,64,512]{3,2,1,0:T(8,128)(2,1)}), bf16[8,2,64,512]{3,2,1,0:T(8,128)(2,1)S(1)}, u32[]{:S(2)}, u32[]{:S(2)}) %all-to-all-start.3) | async-done | bytes 1048608 | tf_op jit(solution)/shard_map/all_to_all | solution.py:328
  59.0 4.2 %all-to-all-start.2 = ((bf16[8,2,64,512]{3,2,1,0:T(8,128)(2,1)}), bf16[8,2,64,512]{3,2,1,0:T(8,128)(2,1)}, u32[]{:S(2)}, u32[]{:S(2)}) async-start(bf16[8,2,64,512]{3,2,1,0:T(8,128)(2,1)} %shard_map.78), calls=%async_computation.2 | async-start | bytes 2097152 | tf_op jit(solution)/shard_map/all_to_all | solution.py:328
  63.2 2.9 %shard_map.77 = bf16[8,2,64,512]{3,2,1,0:T(8,128)(2,1)} custom-call(s32[1]{0:T(128)} %bitcast.core_ref, f32[2,64,512]{2,1,0:T(8,128)} %pad_maximum_fusion.spec_ref, bf16[2,2,2,2,3,64,512]{6,5,4,3,2,1,0:T(8,128)(2,1)} %bitcast.52, bf16[2,2,2,3,64,512]{5,4,3,2,1,0:T(8,128)(2,1)} %collective-permute-done.1.came_ref), custom_call_target="tpu_custom_call" | custom-call | flops 268435456 | bytes 2097152 | tf_op jit(solution)/shard_map/pallas_call | solution.py:159
  66.2 22.6 %all-to-all-done.2.parts_ref = bf16[8,2,64,512]{3,2,1,0:T(8,128)(2,1)} async-done(((bf16[8,2,64,512]{3,2,1,0:T(8,128)(2,1)}), bf16[8,2,64,512]{3,2,1,0:T(8,128)(2,1)}, u32[]{:S(2)}, u32[]{:S(2)}) %all-to-all-start.2) | async-done | bytes 1048608 | tf_op jit(solution)/shard_map/all_to_all | solution.py:328
  88.8 4.2 %all-to-all-start.1 = ((bf16[8,2,64,512]{3,2,1,0:T(8,128)(2,1)}), bf16[8,2,64,512]{3,2,1,0:T(8,128)(2,1)}, u32[]{:S(2)}, u32[]{:S(2)}) async-start(bf16[8,2,64,512]{3,2,1,0:T(8,128)(2,1)} %shard_map.77), calls=%async_computation.1 | async-start | bytes 2097152 | tf_op jit(solution)/shard_map/all_to_all | solution.py:328
  93.2 1.1 collective-permute-done
  95.2 1.2 copy-done.2
  96.5 7.5 %shard_map.80.rest_0_ = f32[1024,1024]{1,0:T(8,128)} custom-call(f32[1]{0:T(128)} %get-tuple-element.12.weight_ref, bf16[8,2,64,512]{3,2,1,0:T(8,128)(2,1)S(1)} %all-to-all-done.3.parts_ref, bf16[1024,1024]{1,0:T(8,128)(2,1)S(1)} %copy-done.1, bf16[4,256,512]{2,1,0:T(8,128)(2,1)S(1)} %copy-done.2), custom_call_target="tpu_custom_call" | custom-call | flops 4294967296 | bytes 5242880 | tf_op jit(solution)/shard_map/pallas_call | solution.py:260
  104.0 9.5 %shard_map.81.rest_0_ = f32[1024,1024]{1,0:T(8,128)} custom-call(f32[1]{0:T(128)} %get-tuple-element.13.weight_ref, bf16[8,2,64,512]{3,2,1,0:T(8,128)(2,1)} %all-to-all-done.2.parts_ref, bf16[1024,1024]{1,0:T(8,128)(2,1)S(1)} %copy-done.1, bf16[4,256,512]{2,1,0:T(8,128)(2,1)S(1)} %copy-done.2, f32[1024,1024]{1,0:T(8,128)} %shard_map.80.rest_0_), custom_call_target="tpu_custom_call" | custom-call | flops 4294967296 | bytes 5242880 | tf_op jit(solution)/shard_map/pallas_call | solution.py:260
  113.5 5.1 %all-to-all-done.1.parts_ref = bf16[8,2,64,512]{3,2,1,0:T(8,128)(2,1)} async-done(((bf16[8,2,64,512]{3,2,1,0:T(8,128)(2,1)}), bf16[8,2,64,512]{3,2,1,0:T(8,128)(2,1)}, u32[]{:S(2)}, u32[]{:S(2)}) %all-to-all-start.1) | async-done | bytes 1048608 | tf_op jit(solution)/shard_map/all_to_all | solution.py:328
  118.5 8.5 %shard_map.82 = bf16[2,8,128,512]{3,2,1,0:T(8,128)(2,1)S(1)} custom-call(f32[1]{0:T(128)} %get-tuple-element.14.weight_ref, bf16[8,2,64,512]{3,2,1,0:T(8,128)(2,1)} %all-to-all-done.1.parts_ref, bf16[1024,1024]{1,0:T(8,128)(2,1)} %constant.46.clone.wave_ref, bf16[4,256,512]{2,1,0:T(8,128)(2,1)S(1)} %copy-done.3, f32[1024,1024]{1,0:T(8,128)} %shard_map.81.rest_0_), custom_call_target="tpu_custom_call" | custom-call | flops 4294967296 | bytes 5242880 | tf_op jit(solution)/shard_map/pallas_call | solution.py:260
  127.3 2.8 %collective-permute-done.2 = bf16[16,64,512]{2,1,0:T(8,128)(2,1)} collective-permute-done((bf16[16,64,512]{2,1,0:T(8,128)(2,1)S(1)}, bf16[16,64,512]{2,1,0:T(8,128)(2,1)}, u32[]{:S(2)}, u32[]{:S(2)}) %collective-permute-start.2) | collective-permute-done | bytes 1048608 | tf_op jit(solution)/shard_map/ppermute | solution.py:344
  130.0 1.5 fusion
  131.6 30.9 %all_to_all.26 = bf16[16,64,512]{2,1,0:T(8,128)(2,1)S(1)} all-to-all(bf16[16,64,512]{2,1,0:T(8,128)(2,1)S(1)} %fusion), channel_id=1, replica_groups=mesh['cond'=2,'kern'=2,'tile'=8] {'kern','tile'}, dimensions={0} | all-to-all | bytes 2097152 | tf_op jit(solution)/shard_map/all_to_all | solution.py:346
  162.8 1.5 collective-permute-done.3
  164.4 0.7 maximum_bitcast_fusion.1
  (32 shorter events, 3.5 us)
Async XLA Ops:
  0.6 6.0 %copy-start = (bf16[1,128,1024]{2,1,0:T(8,128)(2,1)S(1)}, bf16[1,128,1024]{2,1,0:T(8,128)(2,1)}, u32[]{:S(2)}) copy-start(bf16[1,128,1024]{2,1,0:T(8,128)(2,1)} %param.6) | copy-start | bytes 786436
  0.6 3.4 %copy-start.1 = (bf16[1024,1024]{1,0:T(8,128)(2,1)S(1)}, bf16[1024,1024]{1,0:T(8,128)(2,1)}, u32[]{:S(2)}) copy-start(bf16[1024,1024]{1,0:T(8,128)(2,1)} %constant.46.clone.wave_ref) | copy-start | bytes 6291460
  3.5 23.0 %collective-permute-start.1 = (bf16[2,2,2,3,64,512]{5,4,3,2,1,0:T(8,128)(2,1)}, bf16[2,2,2,3,64,512]{5,4,3,2,1,0:T(8,128)(2,1)}, u32[]{:S(2)}, u32[]{:S(2)}) collective-permute-start(bf16[2,2,2,3,64,512]{5,4,3,2,1,0:T(8,128)(2,1)} %dynamic-slice_bitcast_fusion), channel_id=1, source_target_pairs={{0,16},{16,0},{1,17},{17,1},{2,18},{18,2},{3,19},{19,3},{4,20},{20... | collective-permute-start | bytes 4718600 | tf_op jit(solution)/shard_map/ppermute | solution.py:300
  4.0 2.6 %copy-start.5 = (f32[2]{0:T(128)S(1)}, f32[2]{0:T(128)}, u32[]{:S(2)}) copy-start(f32[2]{0:T(128)} %constant.48.clone) | copy-start | bytes 28
  29.4 29.6 %all-to-all-start.3 = ((bf16[8,2,64,512]{3,2,1,0:T(8,128)(2,1)}), bf16[8,2,64,512]{3,2,1,0:T(8,128)(2,1)S(1)}, u32[]{:S(2)}, u32[]{:S(2)}) async-start(bf16[8,2,64,512]{3,2,1,0:T(8,128)(2,1)} %shard_map.79), calls=%async_computation.3 | async-start | bytes 2097152 | tf_op jit(solution)/shard_map/all_to_all | solution.py:328
  59.0 29.8 %all-to-all-start.2 = ((bf16[8,2,64,512]{3,2,1,0:T(8,128)(2,1)}), bf16[8,2,64,512]{3,2,1,0:T(8,128)(2,1)}, u32[]{:S(2)}, u32[]{:S(2)}) async-start(bf16[8,2,64,512]{3,2,1,0:T(8,128)(2,1)} %shard_map.78), calls=%async_computation.2 | async-start | bytes 2097152 | tf_op jit(solution)/shard_map/all_to_all | solution.py:328
  66.2 26.9 %copy-start.4 = (f32[2,12]{1,0:T(2,128)S(1)}, f32[2,12]{1,0:T(2,128)}, u32[]{:S(2)}) copy-start(f32[2,12]{1,0:T(2,128)} %param.8) | copy-start | bytes 292
  88.8 29.7 %all-to-all-start.1 = ((bf16[8,2,64,512]{3,2,1,0:T(8,128)(2,1)}), bf16[8,2,64,512]{3,2,1,0:T(8,128)(2,1)}, u32[]{:S(2)}, u32[]{:S(2)}) async-start(bf16[8,2,64,512]{3,2,1,0:T(8,128)(2,1)} %shard_map.77), calls=%async_computation.1 | async-start | bytes 2097152 | tf_op jit(solution)/shard_map/all_to_all | solution.py:328
  93.1 1.2 collective-permute-start
  95.2 1.2 copy-start.2
  104.0 14.6 %copy-start.3 = (bf16[4,256,512]{2,1,0:T(8,128)(2,1)S(1)}, bf16[4,256,512]{2,1,0:T(8,128)(2,1)}, u32[]{:S(2)}) copy-start(bf16[4,256,512]{2,1,0:T(8,128)(2,1)} %constant.47.clone.back_ref) | copy-start | bytes 3145732
  127.2 2.9 %collective-permute-start.2 = (bf16[16,64,512]{2,1,0:T(8,128)(2,1)S(1)}, bf16[16,64,512]{2,1,0:T(8,128)(2,1)}, u32[]{:S(2)}, u32[]{:S(2)}) collective-permute-start(bf16[16,64,512]{2,1,0:T(8,128)(2,1)S(1)} %dynamic-slice_bitcast_fusion.1), channel_id=1, source_target_pairs={{0,16},{16,0},{1,17},{17,1},{2,18},{18,2},{3,19},{19,3},{4,20},{20... | collective-permute-start | bytes 3145736 | tf_op jit(solution)/shard_map/ppermute | solution.py:344
  162.7 1.6 collective-permute-start.3

commit v2 on v1

--- a/solution.py
+++ b/solution.py
@@ -153,15 +153,12 @@
         (2, conds, None, chunks, None, freqs, count),
         lambda b, own: (0, 0, own[0], 0, which, 0, 0),
     )
-    theirs = pl.BlockSpec(
-        (2, conds, chunks, None, freqs, count), lambda b, own: (0, 0, 0, which, 0, 0)
-    )
     return pl.pallas_call(
         filter_kernel,
         grid_spec=pltpu.PrefetchScalarGridSpec(
             num_scalar_prefetch=1,
             grid=(2,),
-            in_specs=[pl.BlockSpec((2, freqs, count), lambda b, own: (0, 0, 0)), mine, theirs],
+            in_specs=[pl.BlockSpec((2, freqs, count), lambda b, own: (0, 0, 0)), mine, mine],
             out_specs=pl.BlockSpec((owners, 2, freqs, count), lambda b, own: (b, 0, 0, 0)),
         ),
         out_shape=jax.ShapeDtypeStruct((2 * owners, 2, freqs, count), jnp.bfloat16),
@@ -296,8 +293,7 @@
     swap = [(source, 1 - source) for source in range(2)]
     part = kerns // 2
     shares = kernels.reshape(2, conds, 2, part // each, each, freqs, count)
-    came = lax.dynamic_index_in_dim(shares, 1 - core, 2, keepdims=False)
-    came = lax.ppermute(came, "cond", swap)
+    came = lax.ppermute(kernels, "cond", swap).reshape(shares.shape)
     other = lax.ppermute(kernel_weights, "cond", swap)
     weights = jnp.where(
         core == 0,
@@ -306,7 +302,7 @@
     )
     weights = lax.dynamic_slice(weights, (0, core * part), (2 * conds, part)).reshape(items)
     weights = lax.dynamic_slice(weights, (me * each,), (each,))
-    row = jnp.dot(mask[0], wave, preferred_element_type=jnp.float32)
+    row = lax.optimization_barrier(jnp.dot(mask[0], wave, preferred_element_type=jnp.float32))
     row = row.reshape(rows, 2, tile, freqs)
     sign = jnp.asarray([1.0, -1.0], jnp.float32).reshape(1, 2, 1, 1)
     row = (row * sign).astype(jnp.bfloat16)

time: 166 us -> 163 us (0.982)
  blocking collectives: 47 us -> 30.9 us
  waiting for transfers between devices: 56.2 us -> 63.7 us
  starting transfers between devices: 12.8 us -> 20.1 us
  local copies, waits for them, and re-layouts: 7.91 us -> 4.01 us
    all_to_all x1 -> x0, blocking collectives: 16.2 us -> none  [local_items(): cols = lax.all_to_all(row, 'tile', split_axis=0, concat_axis=0, tiled=True)]
    all_to_all x0 -> x1, waiting for transfers between devices: none -> 8.92 us  [local_items(): cols = lax.all_to_all(row, 'tile', split_axis=0, concat_axis=0, tiled=True)]
    all_to_all x0 -> x1, starting transfers between devices: none -> 7.28 us  [local_items(): cols = lax.all_to_all(row, 'tile', split_axis=0, concat_axis=0, tiled=True)]
    squeeze x1 -> x0, local copies, waits for them, and re-layouts: 2.87 us -> none  [local_items(): came = lax.dynamic_index_in_dim(shares, 1 - core, 2, keepdims=False)]
    dot_general x1 -> x0, local copies, waits for them, and re-layouts: 2.56 us -> none  [local_items(): row = jnp.dot(mask[0], wave, preferred_element_type=jnp.float32)]
  transfers between devices with their start and end apart: 7 -> 8, of which waited for: 6 -> 7; matrix products, arithmetic and copies ran while one was open for 4% -> 3% of each run, Pallas kernels for 14% -> 15%
where the time goes in v2:
time: 163 us; the launch traced here: 162 us
  waiting for transfers between devices  63.7 us (39%)
  Pallas kernels  35.1 us (22%)
  blocking collectives  30.9 us (19%)
  starting transfers between devices  20.1 us (12%)
  other arithmetic  4.86 us (3%)
  local copies, waits for them, and re-layouts  4.01 us (2%)
  matrix products  2.94 us (2%)
    all_to_all x3, waiting for transfers between devices, local_items(): lax.all_to_all(sent, 'tile', split_axis=0, concat_axis=0, tiled=True)  49.4 us
    all_to_all x1, blocking collectives, local_items(): lax.all_to_all(total, ('kern', 'tile'), split_axis=0, concat_axis=0, tile...  30.9 us
    pallas_call x3, Pallas kernels, item_round(): pl.pallas_call(functools.partial(item_kernel, first, last), grid=(steps,)...  26.3 us
    all_to_all x3, starting transfers between devices, local_items(): lax.all_to_all(sent, 'tile', split_axis=0, concat_axis=0, tiled=True)  12.1 us
    all_to_all x1, waiting for transfers between devices, local_items(): cols = lax.all_to_all(row, 'tile', split_axis=0, concat_axis=0, tiled=True)  8.92 us
    pallas_call x3, Pallas kernels, filter_round(): pl.pallas_call(filter_kernel, grid_spec=pltpu.PrefetchScalarGridSpec(num_...  8.77 us
    all_to_all x1, starting transfers between devices, local_items(): cols = lax.all_to_all(row, 'tile', split_axis=0, concat_axis=0, tiled=True)  7.28 us
  transfers between devices with their start and end apart: 8, of which 7 were waited for; matrix products, arithmetic and copies ran while one was open for 3% of the time, Pallas kernels for 15%

profile of v2, /device:TPU:0, one launch (start us, length us, event | category | flops | bytes accessed | tf_op | source)
XLA Modules:
  0.0 162.4 jit_solution(6823906165216596013)
XLA Ops:
  1.6 2.5 %convolution_bitcast_fusion = f32[128,1024]{0,1:T(8,128)S(1)} fusion(bf16[1024,1024]{1,0:T(8,128)(2,1)} %constant.42.clone.wave_ref, bf16[1,128,1024]{2,1,0:T(8,128)(2,1)S(1)} %copy-done), kind=kOutput, calls=%fused_computation.3 | convolution fusion | flops 268435456 | bytes 2883584 | tf_op jit(solution)/shard_map/dot_general | solution.py:305
  4.1 0.8 fusion.1
  4.9 7.3 %all-to-all-start = ((bf16[8,128,128]{1,2,0:T(8,128)(2,1)}), bf16[8,128,128]{1,2,0:T(8,128)(2,1)S(1)}, u32[]{:S(2)}, u32[]{:S(2)}) async-start(bf16[8,128,128]{1,2,0:T(8,128)(2,1)} %bitcast.5), calls=%async_computation | async-start | bytes 524288 | tf_op jit(solution)/shard_map/all_to_all | solution.py:310
  12.2 8.9 %all-to-all-done = bf16[8,128,128]{1,2,0:T(8,128)(2,1)S(1)} async-done(((bf16[8,128,128]{1,2,0:T(8,128)(2,1)}), bf16[8,128,128]{1,2,0:T(8,128)(2,1)S(1)}, u32[]{:S(2)}, u32[]{:S(2)}) %all-to-all-start) | async-done | bytes 262176 | tf_op jit(solution)/shard_map/all_to_all | solution.py:310
  21.8 0.7 pad_maximum_fusion.spec_ref
  22.5 2.9 %shard_map.78 = bf16[8,2,64,512]{3,2,1,0:T(8,128)(2,1)} custom-call(s32[1]{0:T(128)} %bitcast.core_ref, f32[2,64,512]{2,1,0:T(8,128)} %pad_maximum_fusion.spec_ref, bf16[2,2,2,2,3,64,512]{6,5,4,3,2,1,0:T(8,128)(2,1)} %bitcast.44, bf16[2,2,2,2,3,64,512]{6,5,4,3,2,1,0:T(8,128)(2,1)} %bitcast.10.came_ref), custom_call_target="tpu_custom_call" | custom-call | flops 268435456 | bytes 2097152 | tf_op jit(solution)/shard_map/pallas_call | solution.py:156
  25.4 3.6 %all-to-all-start.2 = ((bf16[8,2,64,512]{3,2,1,0:T(8,128)(2,1)}), bf16[8,2,64,512]{3,2,1,0:T(8,128)(2,1)S(1)}, u32[]{:S(2)}, u32[]{:S(2)}) async-start(bf16[8,2,64,512]{3,2,1,0:T(8,128)(2,1)} %shard_map.78), calls=%async_computation.2 | async-start | bytes 2097152 | tf_op jit(solution)/shard_map/all_to_all | solution.py:324
  29.0 2.9 %shard_map.79 = bf16[8,2,64,512]{3,2,1,0:T(8,128)(2,1)} custom-call(s32[1]{0:T(128)} %bitcast.core_ref, f32[2,64,512]{2,1,0:T(8,128)} %pad_maximum_fusion.spec_ref, bf16[2,2,2,2,3,64,512]{6,5,4,3,2,1,0:T(8,128)(2,1)} %bitcast.45, bf16[2,2,2,2,3,64,512]{6,5,4,3,2,1,0:T(8,128)(2,1)} %bitcast.10.came_ref), custom_call_target="tpu_custom_call" | custom-call | flops 268435456 | bytes 2097152 | tf_op jit(solution)/shard_map/pallas_call | solution.py:156
  31.9 22.6 %all-to-all-done.2.parts_ref = bf16[8,2,64,512]{3,2,1,0:T(8,128)(2,1)S(1)} async-done(((bf16[8,2,64,512]{3,2,1,0:T(8,128)(2,1)}), bf16[8,2,64,512]{3,2,1,0:T(8,128)(2,1)S(1)}, u32[]{:S(2)}, u32[]{:S(2)}) %all-to-all-start.2) | async-done | bytes 1048608 | tf_op jit(solution)/shard_map/all_to_all | solution.py:324
  54.6 4.3 %all-to-all-start.3 = ((bf16[8,2,64,512]{3,2,1,0:T(8,128)(2,1)}), bf16[8,2,64,512]{3,2,1,0:T(8,128)(2,1)}, u32[]{:S(2)}, u32[]{:S(2)}) async-start(bf16[8,2,64,512]{3,2,1,0:T(8,128)(2,1)} %shard_map.79), calls=%async_computation.3 | async-start | bytes 2097152 | tf_op jit(solution)/shard_map/all_to_all | solution.py:324
  58.8 3.0 %shard_map.77 = bf16[8,2,64,512]{3,2,1,0:T(8,128)(2,1)} custom-call(s32[1]{0:T(128)} %bitcast.core_ref, f32[2,64,512]{2,1,0:T(8,128)} %pad_maximum_fusion.spec_ref, bf16[2,2,2,2,3,64,512]{6,5,4,3,2,1,0:T(8,128)(2,1)} %bitcast.46, bf16[2,2,2,2,3,64,512]{6,5,4,3,2,1,0:T(8,128)(2,1)} %bitcast.10.came_ref), custom_call_target="tpu_custom_call" | custom-call | flops 268435456 | bytes 2097152 | tf_op jit(solution)/shard_map/pallas_call | solution.py:156
  61.8 22.5 %all-to-all-done.3.parts_ref = bf16[8,2,64,512]{3,2,1,0:T(8,128)(2,1)} async-done(((bf16[8,2,64,512]{3,2,1,0:T(8,128)(2,1)}), bf16[8,2,64,512]{3,2,1,0:T(8,128)(2,1)}, u32[]{:S(2)}, u32[]{:S(2)}) %all-to-all-start.3) | async-done | bytes 1048608 | tf_op jit(solution)/shard_map/all_to_all | solution.py:324
  84.3 4.2 %all-to-all-start.1 = ((bf16[8,2,64,512]{3,2,1,0:T(8,128)(2,1)}), bf16[8,2,64,512]{3,2,1,0:T(8,128)(2,1)}, u32[]{:S(2)}, u32[]{:S(2)}) async-start(bf16[8,2,64,512]{3,2,1,0:T(8,128)(2,1)} %shard_map.77), calls=%async_computation.1 | async-start | bytes 2097152 | tf_op jit(solution)/shard_map/all_to_all | solution.py:324
  88.6 1.1 collective-permute-done
  90.6 1.2 copy-done.2
  91.9 8.8 %shard_map.80.rest_0_ = f32[1024,1024]{1,0:T(8,128)} custom-call(f32[1]{0:T(128)} %get-tuple-element.12.weight_ref, bf16[8,2,64,512]{3,2,1,0:T(8,128)(2,1)} %all-to-all-done.3.parts_ref, bf16[1024,1024]{1,0:T(8,128)(2,1)S(1)} %copy-done.1, bf16[4,256,512]{2,1,0:T(8,128)(2,1)S(1)} %copy-done.2), custom_call_target="tpu_custom_call" | custom-call | flops 4294967296 | bytes 5242880 | tf_op jit(solution)/shard_map/pallas_call | solution.py:257
  100.6 9.0 %shard_map.81.rest_0_ = f32[1024,1024]{1,0:T(8,128)} custom-call(f32[1]{0:T(128)} %get-tuple-element.13.weight_ref, bf16[8,2,64,512]{3,2,1,0:T(8,128)(2,1)S(1)} %all-to-all-done.2.parts_ref, bf16[1024,1024]{1,0:T(8,128)(2,1)S(1)} %copy-done.1, bf16[4,256,512]{2,1,0:T(8,128)(2,1)S(1)} %copy-done.2, f32[1024,1024]{1,0:T(8,128)} %shard_map.80.rest_0_), custom_call_target="tpu_custom_call" | custom-call | flops 4294967296 | bytes 5242880 | tf_op jit(solution)/shard_map/pallas_call | solution.py:257
  109.7 4.2 %all-to-all-done.1.parts_ref = bf16[8,2,64,512]{3,2,1,0:T(8,128)(2,1)} async-done(((bf16[8,2,64,512]{3,2,1,0:T(8,128)(2,1)}), bf16[8,2,64,512]{3,2,1,0:T(8,128)(2,1)}, u32[]{:S(2)}, u32[]{:S(2)}) %all-to-all-start.1) | async-done | bytes 1048608 | tf_op jit(solution)/shard_map/all_to_all | solution.py:324
  113.9 1.2 copy-done.3
  115.2 8.5 %shard_map.82 = bf16[2,8,128,512]{3,2,1,0:T(8,128)(2,1)S(1)} custom-call(f32[1]{0:T(128)} %get-tuple-element.14.weight_ref, bf16[8,2,64,512]{3,2,1,0:T(8,128)(2,1)} %all-to-all-done.1.parts_ref, bf16[1024,1024]{1,0:T(8,128)(2,1)} %constant.42.clone.wave_ref, bf16[4,256,512]{2,1,0:T(8,128)(2,1)S(1)} %copy-done.3, f32[1024,1024]{1,0:T(8,128)} %shard_map.81.rest_0_), custom_call_target="tpu_custom_call" | custom-call | flops 4294967296 | bytes 5242880 | tf_op jit(solution)/shard_map/pallas_call | solution.py:257
  123.9 2.8 %collective-permute-done.2 = bf16[16,64,512]{2,1,0:T(8,128)(2,1)} collective-permute-done((bf16[16,64,512]{2,1,0:T(8,128)(2,1)S(1)}, bf16[16,64,512]{2,1,0:T(8,128)(2,1)}, u32[]{:S(2)}, u32[]{:S(2)}) %collective-permute-start.2) | collective-permute-done | bytes 1048608 | tf_op jit(solution)/shard_map/ppermute | solution.py:340
  126.6 1.5 fusion
  128.2 30.9 %all_to_all.25 = bf16[16,64,512]{2,1,0:T(8,128)(2,1)S(1)} all-to-all(bf16[16,64,512]{2,1,0:T(8,128)(2,1)S(1)} %fusion), channel_id=1, replica_groups=mesh['cond'=2,'kern'=2,'tile'=8] {'kern','tile'}, dimensions={0} | all-to-all | bytes 2097152 | tf_op jit(solution)/shard_map/all_to_all | solution.py:342
  159.4 1.5 collective-permute-done.3
  (31 shorter events, 4.6 us)
Async XLA Ops:
  0.6 1.0 copy-start
  0.6 3.4 %copy-start.5 = (f32[2]{0:T(128)S(1)}, f32[2]{0:T(128)}, u32[]{:S(2)}) copy-start(f32[2]{0:T(128)} %constant.44.clone) | copy-start | bytes 28
  0.7 21.9 %collective-permute-start.1 = (bf16[2,2,12,64,512]{4,3,2,1,0:T(8,128)(2,1)}, bf16[2,2,12,64,512]{4,3,2,1,0:T(8,128)(2,1)}, u32[]{:S(2)}, u32[]{:S(2)}) collective-permute-start(bf16[2,2,12,64,512]{4,3,2,1,0:T(8,128)(2,1)} %param.7), channel_id=1, source_target_pairs={{0,16},{16,0},{1,17},{17,1},{2,18},{18,2},{3,19},{19,3},{4,20},{20... | collective-permute-start | bytes 9437192 | tf_op jit(solution)/shard_map/ppermute | solution.py:296
  1.6 19.7 %copy-start.1 = (bf16[1024,1024]{1,0:T(8,128)(2,1)S(1)}, bf16[1024,1024]{1,0:T(8,128)(2,1)}, u32[]{:S(2)}) copy-start(bf16[1024,1024]{1,0:T(8,128)(2,1)} %constant.42.clone.wave_ref) | copy-start | bytes 6291460
  4.9 16.2 %all-to-all-start = ((bf16[8,128,128]{1,2,0:T(8,128)(2,1)}), bf16[8,128,128]{1,2,0:T(8,128)(2,1)S(1)}, u32[]{:S(2)}, u32[]{:S(2)}) async-start(bf16[8,128,128]{1,2,0:T(8,128)(2,1)} %bitcast.5), calls=%async_computation | async-start | bytes 524288 | tf_op jit(solution)/shard_map/all_to_all | solution.py:310
  25.4 29.1 %all-to-all-start.2 = ((bf16[8,2,64,512]{3,2,1,0:T(8,128)(2,1)}), bf16[8,2,64,512]{3,2,1,0:T(8,128)(2,1)S(1)}, u32[]{:S(2)}, u32[]{:S(2)}) async-start(bf16[8,2,64,512]{3,2,1,0:T(8,128)(2,1)} %shard_map.78), calls=%async_computation.2 | async-start | bytes 2097152 | tf_op jit(solution)/shard_map/all_to_all | solution.py:324
  54.6 29.7 %all-to-all-start.3 = ((bf16[8,2,64,512]{3,2,1,0:T(8,128)(2,1)}), bf16[8,2,64,512]{3,2,1,0:T(8,128)(2,1)}, u32[]{:S(2)}, u32[]{:S(2)}) async-start(bf16[8,2,64,512]{3,2,1,0:T(8,128)(2,1)} %shard_map.79), calls=%async_computation.3 | async-start | bytes 2097152 | tf_op jit(solution)/shard_map/all_to_all | solution.py:324
  61.8 26.7 %copy-start.4 = (f32[2,12]{1,0:T(2,128)S(1)}, f32[2,12]{1,0:T(2,128)}, u32[]{:S(2)}) copy-start(f32[2,12]{1,0:T(2,128)} %param.8) | copy-start | bytes 292
  84.3 29.6 %all-to-all-start.1 = ((bf16[8,2,64,512]{3,2,1,0:T(8,128)(2,1)}), bf16[8,2,64,512]{3,2,1,0:T(8,128)(2,1)}, u32[]{:S(2)}, u32[]{:S(2)}) async-start(bf16[8,2,64,512]{3,2,1,0:T(8,128)(2,1)} %shard_map.77), calls=%async_computation.1 | async-start | bytes 2097152 | tf_op jit(solution)/shard_map/all_to_all | solution.py:324
  88.5 1.2 collective-permute-start
  90.6 1.2 copy-start.2
  113.9 1.2 copy-start.3
  123.8 2.9 %collective-permute-start.2 = (bf16[16,64,512]{2,1,0:T(8,128)(2,1)S(1)}, bf16[16,64,512]{2,1,0:T(8,128)(2,1)}, u32[]{:S(2)}, u32[]{:S(2)}) collective-permute-start(bf16[16,64,512]{2,1,0:T(8,128)(2,1)S(1)} %dynamic-slice_bitcast_fusion), channel_id=1, source_target_pairs={{0,16},{16,0},{1,17},{17,1},{2,18},{18,2},{3,19},{19,3},{4,20},{20... | collective-permute-start | bytes 3145736 | tf_op jit(solution)/shard_map/ppermute | solution.py:340
  159.3 1.6 collective-permute-start.3
